TPU v7x, 32 devices: a whole 2x2x4 slice. The times are simulated.
32 devices in a mesh: pop: 8 (over y, x, core), row: 4 (over z).
Axes of the slice: x: 2, y: 2, z: 4, core: 2. Of those that a mesh axis runs over, the one named last changes fastest.
Arguments:
- tokens: bfloat16 [384, 16, 4096], P('pop'), may hold values from -6 to 6
- weight: bfloat16 [14336, 4096], P('row', 'pop'), may hold values from -0.09375 to 0.09375
- bank_in: bfloat16 [4096, 128], P('row'), may hold values from -0.09375 to 0.09375
- bank_out: bfloat16 [14336, 128], P('row'), may hold values from -6 to 6
- fitness: int32 [384], P('pop'), may hold values from 0 to 191
- past_seeds: int32 [384, 2, 8], P('pop'), may hold values from 0 to 127
- new_seeds: int32 [384, 2, 8], P('pop'), may hold values from 0 to 127
Outputs:
- hidden: bfloat16 [384, 16, 14336], P('pop', None, 'row')
- new_weight: bfloat16 [14336, 4096], P('row', 'pop')
All inputs are finite; a program needn't handle non-finite values.
Results may differ from a plain program's by a relative error of at most 0.012.
Values may be sent and summed in bfloat16 or wider, within the bound.
No kernel may reach another device: no remote copies, remote signals or barrier semaphores. Data moves between devices by JAX's collectives and lax.ppermute only.
A program may use at most 128 MiB of HBM per device.

v0:
```python
import jax
import jax.numpy as jnp
from jax import lax
from jax.sharding import PartitionSpec as P

NOISE_SCALE = 0.1
STEP_SCALE = 0.03


def one_hots(seeds, width):
    levels = jnp.arange(width, dtype=jnp.int32)
    out_hits = (seeds[:, 0, :, None] == levels).astype(jnp.float32)
    in_hits = (seeds[:, 1, :, None] == levels).astype(jnp.float32)
    return (out_hits, in_hits)


def shards(tokens, weight, bank_in, bank_out, fitness, past_seeds, new_seeds):
    members = fitness.shape[0]
    overall = members * lax.axis_size("pop")
    width = bank_out.shape[1]
    everyone = lax.all_gather(fitness, "pop", axis=0, tiled=True)
    lower_count = jnp.sum((everyone[None, :] < fitness[:, None]).astype(jnp.float32), axis=1)
    equal_count = jnp.sum((everyone[None, :] == fitness[:, None]).astype(jnp.float32), axis=1)
    centered = (lower_count + 0.5 * (equal_count - 1.0)) / (overall - 1.0) - 0.5
    out_hits, in_hits = one_hots(past_seeds, width)
    local_coupling = STEP_SCALE * jnp.einsum("m,mki,mkj->ij", centered, out_hits, in_hits)
    coupling = lax.psum(local_coupling, "pop")
    full_in = lax.all_gather(bank_in, "row", axis=0, tiled=True)
    left_part = jnp.dot(bank_out.astype(jnp.float32), coupling, precision=lax.Precision.HIGHEST)
    features = tokens.shape[2]
    flat_tokens = tokens.reshape(members * tokens.shape[1], features)
    own_offset = lax.axis_index("pop") * weight.shape[1]
    columns = lax.dynamic_slice_in_dim(full_in, own_offset, weight.shape[1], 0).astype(jnp.float32)
    update = jnp.dot(left_part, columns.T, precision=lax.Precision.HIGHEST)
    new_weight = (weight.astype(jnp.float32) + update).astype(jnp.bfloat16)
    columns = flat_tokens
    base_part = lax.dot_general(
        columns,
        lax.all_gather(new_weight, "pop", axis=1, tiled=True),
        (((1,), (1,)), ((), ())),
        preferred_element_type=jnp.float32,
    )
    projected = jnp.dot(flat_tokens, full_in, preferred_element_type=jnp.float32).reshape(
        members, tokens.shape[1], width
    )
    hidden_hits, feature_hits = one_hots(new_seeds, width)
    mixing = jnp.einsum("mkb,mkc->mbc", feature_hits, hidden_hits)
    low_term = (NOISE_SCALE * jnp.einsum("mtb,mbc->mtc", projected, mixing)).astype(jnp.bfloat16)
    extra = lax.dot_general(
        low_term.reshape(flat_tokens.shape[0], width),
        bank_out,
        (((1,), (1,)), ((), ())),
        preferred_element_type=jnp.float32,
    )
    hidden = (
        (base_part + extra).astype(jnp.bfloat16).reshape(members, tokens.shape[1], weight.shape[0])
    )
    return (hidden, new_weight)


def solution(mesh):
    placed = (
        P("pop", None, None),
        P("row", "pop"),
        P("row", None),
        P("row", None),
        P("pop"),
        P("pop", None, None),
        P("pop", None, None),
    )
    return jax.shard_map(
        shards,
        mesh=mesh,
        in_specs=placed,
        out_specs=(P("pop", None, "row"), P("row", "pop")),
        check_vma=False,
    )
```

profile of v0, /device:TPU:0, one launch (start us, length us, event | category | flops | bytes accessed | tf_op | source)
XLA Modules:
  0.0 272.2 jit_solution(11762700354457997980)
XLA Ops:
  8.0 0.0 copy-start
  8.0 0.0 all-reduce.3.cloned.1.call-start
  8.1 1.3 dynamic-slice
  10.0 0.9 dynamic-update-slice
  10.9 9.5 %all-reduce = s32[384]{0:T(512)S(1)} all-reduce(s32[384]{0:T(512)S(1)} %dynamic-update-slice), channel_id=1, replica_groups=mesh['pop'=8,'row'=4] {'pop'}, use_global_device_ids=true, to_apply=%add | all-reduce | flops 384 | bytes 3072
  20.4 0.8 convert_reduce_fusion
  21.2 0.7 slice_bitcast_fusion.3
  21.9 0.1 copy.13
  22.0 0.1 copy.14
  22.1 1.0 fusion.16
  23.1 0.0 all-reduce.3.cloned.1.call-update
  23.2 0.0 all-gather.3.cloned.1.call-start
  23.2 0.5 all-gather.3.cloned.1.call-update
  23.7 0.0 all-gather.5.cloned.1.call-start
  23.8 52.4 %all-reduce.3.cloned.1.call-done = f32[128,128]{1,0:T(8,128)} async-done(((f32[128,128]{1,0:T(8,128)}), f32[128,128]{1,0:T(8,128)}) %all-reduce.3.cloned.1.call-update) | async-done | bytes 65552 | tf_op jit(solution)/shard_map/psum | solution.py:27
  76.2 0.0 copy-done
  76.2 1.8 fusion.31
  77.9 0.0 copy-start.1
  77.9 0.0 all-gather.3.cloned.1.call-done
  78.0 6.2 %add_convert_fusion = bf16[3584,512]{1,0:T(8,128)(2,1)} fusion(bf16[3584,512]{1,0:T(8,128)(2,1)} %param.8, f32[128,3584]{1,0:T(8,128)S(1)} %fusion.31, bf16[4096,128]{1,0:T(8,128)(2,1)} %all-gather.3.cloned.1.call-done, s32[]{:T(128)S(6)} %select_n.3), kind=kOutput, calls=%fused_computation.2 | convolution fusion | flops 2824077312 | bytes 9306116 | tf_op jit(solution)/shard_map/dot_general | solution.py:34
  84.2 0.0 all-gather.5.cloned.1.call-update
  84.2 0.0 copy-done.1
  84.2 0.1 copy.15
  84.3 0.1 copy.16
  84.4 6.3 %fusion.11 = bf16[48,16,128]{2,1,0:T(8,128)(2,1)S(1)} fusion(bf16[48,16,4096]{2,1,0:T(8,128)(2,1)} %param.7, bf16[4096,128]{1,0:T(8,128)(2,1)} %all-gather.3.cloned.1.call-done, s32[48,8]{1,0:T(8,128)S(1)} %copy.16, s32[48,8]{1,0:T(8,128)S(1)} %copy.15), kind=kOutput, calls=%fused_computation.7 | convolution fusion | flops 843350016 | bytes 7539712 | tf_op jit(solution)/shard_map/mtb,mbc->mtc/dot_general | solution.py:48
  90.7 141.8 %all-gather.5.cloned.1.call-done = bf16[3584,4096]{1,0:T(8,128)(2,1)} async-done(((bf16[3584,512]{1,0:T(8,128)(2,1)}), bf16[3584,4096]{1,0:T(8,128)(2,1)}) %all-gather.5.cloned.1.call-update) | async-done | bytes 29360144 | tf_op jit(solution)/shard_map/all_gather | solution.py:39
  232.5 28.2 %fusion.32 = f32[3584,768]{0,1:T(8,128)S(1)} fusion(bf16[3584,4096]{1,0:T(8,128)(2,1)} %all-gather.5.cloned.1.call-done, bf16[768,4096]{1,0:T(8,128)(2,1)} %bitcast.34), kind=kOutput, calls=%fused_computation.33 | convolution fusion | flops 22548578304 | bytes 46661632 | tf_op jit(solution)/shard_map/dot_general | solution.py:37
  260.7 4.0 %fusion = bf16[768,3584]{1,0:T(8,128)(2,1)} fusion(f32[3584,768]{0,1:T(8,128)S(1)} %fusion.32, bf16[768,128]{1,0:T(8,128)(2,1)S(1)} %bitcast.33, bf16[3584,128]{1,0:T(8,128)(2,1)S(1)} %copy-done), kind=kOutput, calls=%fused_computation.1 | convolution fusion | flops 710148096 | bytes 17629184 | tf_op jit(solution)/shard_map/dot_general | solution.py:49
  (3 shorter events, 0.0 us)
Async XLA Ops:
  8.0 68.2 %copy-start = (bf16[3584,128]{1,0:T(8,128)(2,1)S(1)}, bf16[3584,128]{1,0:T(8,128)(2,1)}, u32[]{:S(2)}) copy-start(bf16[3584,128]{1,0:T(8,128)(2,1)} %param.10) | copy-start | bytes 2752516
  8.0 68.1 %all-reduce.3.cloned.1.call-start = ((), (), s32[]{:S(2)}) async-start(), calls=%async_computation | async-start | bytes 131072 | tf_op jit(solution)/shard_map/psum | solution.py:27
  23.2 54.8 %all-gather.3.cloned.1.call-start = ((), (), s32[]{:S(2)}) async-start(), calls=%async_computation.1 | async-start | bytes 1310720 | tf_op jit(solution)/shard_map/all_gather | solution.py:28
  23.7 208.8 %all-gather.5.cloned.1.call-start = ((), (), s32[]{:S(2)}) async-start(), calls=%async_computation.2 | async-start | bytes 33030144 | tf_op jit(solution)/shard_map/all_gather | solution.py:39
  77.9 6.3 %copy-start.1 = (s32[48,2,8]{0,2,1:T(8,128)S(1)}, s32[48,2,8]{0,2,1:T(8,128)}, u32[]{:S(2)}) copy-start(s32[48,2,8]{0,2,1:T(8,128)} %param.13) | copy-start | bytes 9220
Sparse Core Ops, SparseCore 0:
  23.3 52.8 all-reduce.2
  84.3 148.1 all-gather.4
Sparse Core Ops, SparseCore 1:
  25.2 27.5 all-gather.2
where the time goes:
time: 272 us
  waiting for transfers between devices  195 us (72%)
  matrix products  47.6 us (18%)
  between operations  16.2 us (6%)
  blocking collectives  9.49 us (3%)
  local copies, waits for them, and re-layouts  3.23 us (1%)
    all_gather x1, waiting for transfers between devices, shards(): lax.all_gather(new_weight, 'pop', axis=1, tiled=True)  142 us
    psum x1, waiting for transfers between devices, shards(): coupling = lax.psum(local_coupling, 'pop')  52.4 us
    dot_general x1, matrix products, shards(): lax.dot_general(columns, lax.all_gather(new_weight, 'pop', axis=1, tiled=...  28.2 us
    unnamed x1, blocking collectives  9.49 us
    dot_general x1, matrix products, shards(): jnp.einsum('mtb,mbc->mtc', projected, mixing)  6.34 us
    dot_general x1, matrix products, shards(): update = jnp.dot(left_part, columns.T, precision=lax.Precision.HIGHEST)  6.22 us
  transfers between devices with their start and end apart: 3, of which 2 were waited for; matrix products, arithmetic and copies ran while one was open for 3% of the time, Pallas kernels for 0%

commit v1 on v0

--- a/solution.py
+++ b/solution.py
@@ -24,7 +24,7 @@
     centered = (lower_count + 0.5 * (equal_count - 1.0)) / (overall - 1.0) - 0.5
     out_hits, in_hits = one_hots(past_seeds, width)
     local_coupling = STEP_SCALE * jnp.einsum("m,mki,mkj->ij", centered, out_hits, in_hits)
-    coupling = lax.psum(local_coupling, "pop")
+    coupling = jnp.sum(lax.all_gather(local_coupling, "pop"), axis=0)
     full_in = lax.all_gather(bank_in, "row", axis=0, tiled=True)
     left_part = jnp.dot(bank_out.astype(jnp.float32), coupling, precision=lax.Precision.HIGHEST)
     features = tokens.shape[2]

time: 272 us -> 234 us (0.86)
  waiting for transfers between devices: 195 us -> 150 us
  blocking collectives: 9.49 us -> 18.7 us
    psum x1 -> x0, waiting for transfers between devices: 52.4 us -> none  [shards(): coupling = lax.psum(local_coupling, 'pop')]
    all_gather x0 -> x1, blocking collectives: none -> 9.21 us  [shards(): coupling = jnp.sum(lax.all_gather(local_coupling, 'pop'), axis=0)]
    all_gather x1, waiting for transfers between devices: 0.03 us -> 7.91 us  [shards(): full_in = lax.all_gather(bank_in, 'row', axis=0, tiled=True)]
  transfers between devices with their start and end apart: 3 -> 2, of which waited for: 2 -> 2; matrix products, arithmetic and copies ran while one was open for 3% -> 5% of each run, Pallas kernels for 0% -> 0%
where the time goes in v1:
time: 234 us
  waiting for transfers between devices  150 us (64%)
  matrix products  46.1 us (20%)
  blocking collectives  18.7 us (8%)
  between operations  14.8 us (6%)
  local copies, waits for them, and re-layouts  2.99 us (1%)
    all_gather x1, waiting for transfers between devices, shards(): lax.all_gather(new_weight, 'pop', axis=1, tiled=True)  142 us
    dot_general x1, matrix products, shards(): lax.dot_general(columns, lax.all_gather(new_weight, 'pop', axis=1, tiled=...  28.2 us
    unnamed x1, blocking collectives  9.49 us
    all_gather x1, blocking collectives, shards(): coupling = jnp.sum(lax.all_gather(local_coupling, 'pop'), axis=0)  9.21 us
    all_gather x1, waiting for transfers between devices, shards(): full_in = lax.all_gather(bank_in, 'row', axis=0, tiled=True)  7.91 us
    dot_general x1, matrix products, shards(): jnp.einsum('mtb,mbc->mtc', projected, mixing)  6.35 us
    dot_general x1, matrix products, shards(): update = jnp.dot(left_part, columns.T, precision=lax.Precision.HIGHEST)  6.2 us
  transfers between devices with their start and end apart: 2, of which 2 were waited for; matrix products, arithmetic and copies ran while one was open for 5% of the time, Pallas kernels for 0%

profile of v1, /device:TPU:0, one launch (start us, length us, event | category | flops | bytes accessed | tf_op | source)
XLA Modules:
  0.0 233.9 jit_solution(12375233782503668630)
XLA Ops:
  7.2 0.0 copy-start
  7.2 0.0 all-gather.4.cloned.1.call-start
  7.2 0.7 all-gather.4.cloned.1.call-update
  7.9 0.0 all-gather.6.cloned.1.call-start
  8.0 1.2 dynamic-slice
  9.9 0.9 dynamic-update-slice
  10.7 9.5 %all-reduce = s32[384]{0:T(512)S(1)} all-reduce(s32[384]{0:T(512)S(1)} %dynamic-update-slice), channel_id=1, replica_groups=mesh['pop'=8,'row'=4] {'pop'}, use_global_device_ids=true, to_apply=%add | all-reduce | flops 384 | bytes 3072
  20.2 0.8 convert_reduce_fusion
  21.1 0.7 slice_bitcast_fusion.3
  21.8 0.4 fusion.16
  22.2 9.2 %all-gather = f32[1024,128]{1,0:T(8,128)S(1)} all-gather(f32[128,128]{1,0:T(8,128)S(1)} %fusion.16), channel_id=2, replica_groups=mesh['pop'=8,'row'=4] {'pop'}, dimensions={0}, use_global_device_ids=true | all-gather | bytes 589824 | tf_op jit(solution)/shard_map/all_gather | solution.py:27
  31.4 0.0 copy-done
  31.4 0.9 fusion.31
  32.4 0.0 copy-start.1
  32.4 7.9 %all-gather.4.cloned.1.call-done = bf16[4096,128]{1,0:T(8,128)(2,1)} async-done(((bf16[1024,128]{1,0:T(8,128)(2,1)}), bf16[4096,128]{1,0:T(8,128)(2,1)}) %all-gather.4.cloned.1.call-update) | async-done | bytes 1048592 | tf_op jit(solution)/shard_map/all_gather | solution.py:28
  40.3 6.2 %add_convert_fusion = bf16[3584,512]{1,0:T(8,128)(2,1)} fusion(bf16[3584,512]{1,0:T(8,128)(2,1)} %param.8, f32[128,3584]{1,0:T(8,128)S(1)} %fusion.31, bf16[4096,128]{1,0:T(8,128)(2,1)} %all-gather.4.cloned.1.call-done, s32[]{:T(128)S(6)} %select_n.3), kind=kOutput, calls=%fused_computation.2 | convolution fusion | flops 2824077312 | bytes 9306116 | tf_op jit(solution)/shard_map/dot_general | solution.py:34
  46.5 0.0 all-gather.6.cloned.1.call-update
  46.5 0.0 copy-done.1
  46.5 0.1 copy.11
  46.6 0.1 copy.12
  46.7 6.3 %fusion.11 = bf16[48,16,128]{2,1,0:T(8,128)(2,1)S(1)} fusion(bf16[48,16,4096]{2,1,0:T(8,128)(2,1)} %param.7, bf16[4096,128]{1,0:T(8,128)(2,1)} %all-gather.4.cloned.1.call-done, s32[48,8]{1,0:T(8,128)S(1)} %copy.12, s32[48,8]{1,0:T(8,128)S(1)} %copy.11), kind=kOutput, calls=%fused_computation.7 | convolution fusion | flops 843350016 | bytes 7539712 | tf_op jit(solution)/shard_map/mtb,mbc->mtc/dot_general | solution.py:48
  53.0 141.8 %all-gather.6.cloned.1.call-done = bf16[3584,4096]{1,0:T(8,128)(2,1)} async-done(((bf16[3584,512]{1,0:T(8,128)(2,1)}), bf16[3584,4096]{1,0:T(8,128)(2,1)}) %all-gather.6.cloned.1.call-update) | async-done | bytes 29360144 | tf_op jit(solution)/shard_map/all_gather | solution.py:39
  194.8 28.2 %fusion.32 = f32[3584,768]{0,1:T(8,128)S(1)} fusion(bf16[3584,4096]{1,0:T(8,128)(2,1)} %all-gather.6.cloned.1.call-done, bf16[768,4096]{1,0:T(8,128)(2,1)} %bitcast.36), kind=kOutput, calls=%fused_computation.33 | convolution fusion | flops 22548578304 | bytes 46661632 | tf_op jit(solution)/shard_map/dot_general | solution.py:37
  223.0 4.0 %fusion = bf16[768,3584]{1,0:T(8,128)(2,1)} fusion(f32[3584,768]{0,1:T(8,128)S(1)} %fusion.32, bf16[768,128]{1,0:T(8,128)(2,1)S(1)} %bitcast.35, bf16[3584,128]{1,0:T(8,128)(2,1)S(1)} %copy-done), kind=kOutput, calls=%fused_computation.1 | convolution fusion | flops 710148096 | bytes 17629184 | tf_op jit(solution)/shard_map/dot_general | solution.py:49
  (4 shorter events, 0.0 us)
Async XLA Ops:
  7.2 24.3 %copy-start = (bf16[3584,128]{1,0:T(8,128)(2,1)S(1)}, bf16[3584,128]{1,0:T(8,128)(2,1)}, u32[]{:S(2)}) copy-start(bf16[3584,128]{1,0:T(8,128)(2,1)} %param.10) | copy-start | bytes 2752516
  7.2 33.1 %all-gather.4.cloned.1.call-start = ((), (), s32[]{:S(2)}) async-start(), calls=%async_computation | async-start | bytes 1310720 | tf_op jit(solution)/shard_map/all_gather | solution.py:28
  7.9 186.9 %all-gather.6.cloned.1.call-start = ((), (), s32[]{:S(2)}) async-start(), calls=%async_computation.1 | async-start | bytes 33030144 | tf_op jit(solution)/shard_map/all_gather | solution.py:39
  32.4 14.1 %copy-start.1 = (s32[48,2,8]{0,2,1:T(8,128)S(1)}, s32[48,2,8]{0,2,1:T(8,128)}, u32[]{:S(2)}) copy-start(s32[48,2,8]{0,2,1:T(8,128)} %param.13) | copy-start | bytes 9220
Sparse Core Ops, SparseCore 0:
  9.6 30.6 all-gather.3
  46.6 148.1 all-gather.5
